TPU v7x, 32 devices: a whole 2x2x4 slice. The times are simulated.
32 devices in a mesh: dp: 32 (over z, y, x, core), tensor: 1.
Axes of the slice: x: 2, y: 2, z: 4, core: 2. Of those that a mesh axis runs over, the one named last changes fastest.
Arguments:
- activations: bfloat16 [384, 8192], P('dp', 'tensor'), may hold values from -400 to 400, as said below
- weight: bfloat16 [8192, 28672], P('dp', 'tensor'), may hold values from -0.0625 to 0.0625
Outputs:
- channel_mean: float32 [8192], P('dp')
- column_errors: float32 [4, 28672], P(None, ('tensor', 'dp'))
- errors: float32 [4], replicated
Inputs may be any that keep to these rules, and one draw needn't show every extreme that they name: activations and weight are finite real values within the ranges stated above.
All inputs are finite; a program needn't handle non-finite values.
Results may differ from a plain program's by a relative error of at most 0.0012.
The roundings to bfloat16 on the way count: a program that leaves them out, or rounds other values in their place, can miss the bound.
Values may be sent and summed in bfloat16 or wider, within the bound.
A program may use at most 128 MiB of HBM per device.

v0:
```python
import functools
import math

import jax
import jax.numpy as jnp
from jax import lax
from jax.experimental import pallas as pl
from jax.experimental.pallas import tpu as pltpu
from jax.sharding import PartitionSpec as P

GROUP = 128
GRID = 4
LANES = 128
TILE = 256
SINE = (
    6.283182818832115,
    -41.34142141640176,
    81.59618421926638,
    -76.5801034177733,
    41.205405703161745,
    -12.271277356143528,
)


def sine_of_turns(r):
    square = r * r
    value = SINE[-1] * square + SINE[-2]
    for c in SINE[-3::-1]:
        value = value * square + c
    return value * r


def partial_kernel(steps, a_ref, w_ref, s_ref, out_ref, acc, change):
    step = pl.program_id(0)
    depth, width = w_ref.shape

    @pl.when(step == 0)
    def _():
        acc[...] = jnp.zeros_like(acc)

    def tile(start, size):
        def columns(offset, length):
            if isinstance(start, int):
                return pl.ds(start + offset, length)
            return pl.ds(pl.multiple_of(start + offset, LANES), length)

        for k in range(GRID):
            for g in range(depth // GROUP):
                rows = pl.ds(g * GROUP, GROUP)
                for c in range(0, size, LANES):
                    lanes = min(LANES, size - c)
                    w = w_ref[rows, columns(c, lanes)].astype(jnp.float32)
                    scaled = w * s_ref[k, rows, :lanes]
                    top = jnp.max(jnp.abs(scaled), axis=0, keepdims=True)
                    quant_step = (top + 1e-06) / 7.0
                    v = scaled * (1.0 / quant_step)
                    wave = sine_of_turns(v - jnp.round(v))
                    wave = wave * (quant_step * (0.5 / math.pi))
                    dequant = w - wave * s_ref[GRID + k, rows, :lanes]
                    dequant = dequant.astype(jnp.bfloat16).astype(jnp.float32)
                    change[k, rows, pl.ds(c, lanes)] = (dequant - w).astype(jnp.bfloat16)
            acc[k, :, columns(0, size)] += jnp.dot(
                a_ref[...], change[k, :, pl.ds(0, size)], preferred_element_type=jnp.float32
            )

    whole = width // TILE
    if whole:

        @pl.loop(0, whole)
        def _(i):
            tile(i * TILE, TILE)

    if width % TILE:
        tile(whole * TILE, width % TILE)

    @pl.when(step == steps - 1)
    def _():
        for k in range(GRID):
            out_ref[k] = acc[k].astype(out_ref.dtype)


def partial_residue(tokens, columns, table, depth, kind):
    count, channels = tokens.shape
    width = columns.shape[1]
    steps = channels // depth
    return pl.pallas_call(
        functools.partial(partial_kernel, steps),
        grid=(steps,),
        out_shape=jax.ShapeDtypeStruct((GRID, count, width), kind),
        in_specs=[
            pl.BlockSpec((count, depth), lambda i: (0, i)),
            pl.BlockSpec((depth, width), lambda i: (i, 0)),
            pl.BlockSpec((2 * GRID, depth, LANES), lambda i: (0, i, 0)),
        ],
        out_specs=pl.BlockSpec((GRID, count, width), lambda i: (0, 0, 0)),
        scratch_shapes=[
            pltpu.VMEM((GRID, count, width), jnp.float32),
            pltpu.VMEM((GRID, depth, min(TILE, -(-width // LANES) * LANES)), jnp.bfloat16),
        ],
        compiler_params=pltpu.CompilerParams(
            dimension_semantics=("arbitrary",), vmem_limit_bytes=48 << 20
        ),
        cost_estimate=pl.CostEstimate(
            flops=30 * GRID * channels * width * 16,
            bytes_accessed=4 * channels * width,
            transcendentals=0,
        ),
    )(tokens, columns, table)


def on_device(activations, weight):
    n = lax.axis_size("dp")
    half = n // 2
    me = lax.axis_index("dp")
    side, place = me // half, me % half
    groups = [list(range(half)), list(range(half, n))]
    across = [(i, (i + half) % n) for i in range(n)]

    widened = lax.all_gather(activations, "tensor", axis=1, tiled=True)
    own_tokens, channels = widened.shape
    mine = channels // 2
    token_count = own_tokens * n
    kept = lax.dynamic_slice_in_dim(widened, side * mine, mine, axis=1)
    away = lax.dynamic_slice_in_dim(widened, (1 - side) * mine, mine, axis=1)
    other = lax.ppermute(away, "dp", across)
    first = side == 0
    pair = jnp.concatenate([jnp.where(first, kept, other), jnp.where(first, other, kept)], axis=0)
    tokens = lax.all_gather(pair, "dp", axis=0, tiled=True, axis_index_groups=groups)

    width = weight.shape[1]
    away_weight = lax.dynamic_slice_in_dim(weight, (1 - side) * (width // 2), width // 2, axis=1)
    kept_weight = lax.dynamic_slice_in_dim(weight, side * (width // 2), width // 2, axis=1)
    exchange = functools.partial(
        lax.all_to_all, axis_name="dp", split_axis=1, concat_axis=0, tiled=True, axis_index_groups=groups
    )
    away_columns = exchange(away_weight)
    kept_columns = exchange(kept_weight)

    half_mean = jnp.sum(jnp.abs(tokens.astype(jnp.float32)), axis=0) / token_count + 1e-06
    other_mean = lax.ppermute(half_mean, "dp", across)
    ratios = jnp.arange(GRID, dtype=jnp.float32) / GRID
    raw = jnp.exp(ratios[:, None] * jnp.log(half_mean)[None, :])
    raw_other = jnp.exp(ratios[:, None] * jnp.log(other_mean)[None, :])
    top = jnp.maximum(jnp.max(raw, axis=1, keepdims=True), jnp.max(raw_other, axis=1, keepdims=True))
    bottom = jnp.minimum(jnp.min(raw, axis=1, keepdims=True), jnp.min(raw_other, axis=1, keepdims=True))
    scales = raw / jnp.sqrt(top * bottom)
    table = jnp.concatenate([scales, 1.0 / scales], axis=0)
    table = jnp.broadcast_to(table[:, :, None], (2 * GRID, mine, LANES))

    depth = weight.shape[0]
    away_part = partial_residue(tokens, away_columns, table, depth, jnp.bfloat16)
    arrived = lax.ppermute(away_part, "dp", across)
    own_part = partial_residue(tokens, kept_columns, table, depth, jnp.float32)
    residue = own_part + arrived.astype(jnp.float32)
    column_sums = jnp.sum(residue * residue, axis=1)

    totals = lax.psum(jnp.sum(column_sums, axis=1), ("dp", "tensor"))
    errors = totals / (token_count * width * lax.axis_size("tensor"))
    column_errors = column_sums / token_count
    own_mean = lax.dynamic_slice_in_dim(half_mean, place * depth, depth)
    return (own_mean, column_errors, errors)


def solution(mesh):
    placed = (P("dp", "tensor"), P("dp", "tensor"))
    return jax.shard_map(
        on_device,
        mesh=mesh,
        in_specs=placed,
        out_specs=(P("dp"), P(None, ("tensor", "dp")), P()),
        check_vma=False,
    )
```

profile of v0, /device:TPU:0, one launch (start us, length us, event | category | flops | bytes accessed | tf_op | source)
XLA Modules:
  0.0 574.7 jit_solution(3733999944464989298)
XLA Ops:
  7.2 10.6 %constant_dynamic-slice_fusion = (bf16[256,14336]{1,0:T(8,128)(2,1)}, bf16[256,14336]{1,0:T(8,128)(2,1)}) fusion(bf16[256,28672]{1,0:T(8,128)(2,1)} %param.3, s32[]{:T(128)S(6)} %select_n.47, s32[]{:T(128)S(6)} %select_n.46), kind=kLoop, calls=%fused_computation.18 | loop fusion | bytes 29360136 | tf_op jit(solution)/shard_map/dynamic_slice | solution.py:131
  17.8 10.0 %copy.10 = bf16[256,14336]{0,1:T(8,128)(2,1)} copy(bf16[256,14336]{1,0:T(8,128)(2,1)} %get-tuple-element.11) | data formatting | bytes 14680064
  27.8 6.4 %all-to-all-start.1 = ((bf16[256,16,896]{0,2,1:T(8,128)(2,1)}), bf16[256,16,896]{0,2,1:T(8,128)(2,1)}, u32[]{:S(2)}, u32[]{:S(2)}) async-start(bf16[256,16,896]{0,2,1:T(8,128)(2,1)} %bitcast.8), calls=%async_computation.1 | async-start | bytes 14680064 | tf_op jit(solution)/shard_map/all_to_all | solution.py:136
  34.2 10.1 %copy.9 = bf16[256,14336]{0,1:T(8,128)(2,1)} copy(bf16[256,14336]{1,0:T(8,128)(2,1)} %get-tuple-element.12) | data formatting | bytes 14680064
  44.3 101.7 %all-to-all-done.1 = bf16[256,16,896]{0,2,1:T(8,128)(2,1)} async-done(((bf16[256,16,896]{0,2,1:T(8,128)(2,1)}), bf16[256,16,896]{0,2,1:T(8,128)(2,1)}, u32[]{:S(2)}, u32[]{:S(2)}) %all-to-all-start.1) | async-done | bytes 7340064 | tf_op jit(solution)/shard_map/all_to_all | solution.py:136
  146.1 5.8 %all-to-all-start = ((bf16[256,16,896]{0,2,1:T(8,128)(2,1)}), bf16[256,16,896]{0,2,1:T(8,128)(2,1)}, u32[]{:S(2)}, u32[]{:S(2)}) async-start(bf16[256,16,896]{0,2,1:T(8,128)(2,1)} %bitcast.7), calls=%async_computation | async-start | bytes 14680064 | tf_op jit(solution)/shard_map/all_to_all | solution.py:137
  151.9 2.7 collective-permute-start
  154.6 111.8 %collective-permute-done = bf16[12,4096]{1,0:T(8,128)(2,1)S(1)} collective-permute-done((bf16[12,4096]{1,0:T(8,128)(2,1)S(1)}, bf16[12,4096]{1,0:T(8,128)(2,1)S(1)}, u32[]{:S(2)}, u32[]{:S(2)}) %collective-permute-start) | collective-permute-done | bytes 98336 | tf_op jit(solution)/shard_map/ppermute | solution.py:125
  266.5 0.7 pad_maximum_fusion
  267.2 33.1 %all-gather.2.cloned.1.call-done.a_ref = bf16[384,4096]{1,0:T(8,128)(2,1)} async-done(((bf16[24,4096]{1,0:T(8,128)(2,1)}), bf16[384,4096]{1,0:T(8,128)(2,1)}) %all-gather.2.cloned.1.call-update) | async-done | bytes 3145744 | tf_op jit(solution)/shard_map/all_gather | solution.py:128
  300.3 2.6 abs_reduce_fusion
  302.9 2.5 collective-permute-start.1
  305.4 2.4 collective-permute-done.1
  308.2 11.2 %copy.8 = bf16[16,256,896]{2,1,0:T(8,128)(2,1)} copy(bf16[16,256,896]{1,2,0:T(8,128)(2,1)} %bitcast.4) | data formatting | bytes 14680064 | tf_op jit(solution)/shard_map/all_to_all | solution.py:136
  319.4 6.2 %broadcast_in_dim.2.s_ref = f32[8,4096,128]{2,1,0:T(8,128)} broadcast(f32[8,4096]{1,0:T(8,128)S(1)} %pad_maximum_fusion.1), dimensions={0,1} | broadcast | bytes 16908288 | tf_op jit(solution)/shard_map/broadcast_in_dim | solution.py:148
  325.7 78.2 %shard_map.50 = bf16[4,384,896]{2,1,0:T(8,128)(2,1)} custom-call(bf16[384,4096]{1,0:T(8,128)(2,1)S(1)} %copy-done, bf16[4096,896]{1,0:T(8,128)(2,1)} %bitcast.6, f32[8,4096,128]{2,1,0:T(8,128)} %broadcast_in_dim.2.s_ref), custom_call_target="tpu_custom_call" | custom-call | flops 7046430720 | bytes 14680064 | tf_op jit(solution)/shard_map/pallas_call | solution.py:86
  403.9 2.2 collective-permute-start.2
  406.1 0.6 dynamic_slice.17
  406.8 11.2 %copy.6 = bf16[16,256,896]{2,1,0:T(8,128)(2,1)} copy(bf16[16,256,896]{1,2,0:T(8,128)(2,1)} %bitcast.1) | data formatting | bytes 14680064 | tf_op jit(solution)/shard_map/all_to_all | solution.py:137
  418.0 79.1 %shard_map.49 = f32[4,384,896]{2,1,0:T(8,128)} custom-call(bf16[384,4096]{1,0:T(8,128)(2,1)S(1)} %copy-done, bf16[4096,896]{1,0:T(8,128)(2,1)} %bitcast.9, f32[8,4096,128]{2,1,0:T(8,128)} %broadcast_in_dim.2.s_ref), custom_call_target="tpu_custom_call" | custom-call | flops 7046430720 | bytes 14680064 | tf_op jit(solution)/shard_map/pallas_call | solution.py:86
  497.1 27.6 %collective-permute-done.2 = bf16[4,384,896]{2,1,0:T(8,128)(2,1)} collective-permute-done((bf16[4,384,896]{2,1,0:T(8,128)(2,1)}, bf16[4,384,896]{2,1,0:T(8,128)(2,1)}, u32[]{:S(2)}, u32[]{:S(2)}) %collective-permute-start.2) | collective-permute-done | bytes 2752544 | tf_op jit(solution)/shard_map/ppermute | solution.py:152
  524.7 4.4 fusion
  529.1 37.6 %psum.7 = f32[4]{0:T(128)S(1)} all-reduce(f32[4]{0:T(128)S(1)} %get-tuple-element.3), channel_id=1, replica_groups=mesh['dp'=32,'tensor'=1] {'dp','tensor'}, use_global_device_ids=true, to_apply=%region_7.8 | all-reduce | flops 4 | bytes 32 | tf_op jit(solution)/shard_map/psum | solution.py:157
  567.3 0.6 broadcast_multiply_fusion
  (17 shorter events, 1.1 us)
Async XLA Ops:
  27.8 118.3 %all-to-all-start.1 = ((bf16[256,16,896]{0,2,1:T(8,128)(2,1)}), bf16[256,16,896]{0,2,1:T(8,128)(2,1)}, u32[]{:S(2)}, u32[]{:S(2)}) async-start(bf16[256,16,896]{0,2,1:T(8,128)(2,1)} %bitcast.8), calls=%async_computation.1 | async-start | bytes 14680064 | tf_op jit(solution)/shard_map/all_to_all | solution.py:136
  146.1 5.8 %copy-start.1 = (bf16[12,8192]{1,0:T(8,128)(2,1)S(1)}, bf16[12,8192]{1,0:T(8,128)(2,1)}, u32[]{:S(2)}) copy-start(bf16[12,8192]{1,0:T(8,128)(2,1)} %param.2) | copy-start | bytes 589828
  146.1 260.7 %all-to-all-start = ((bf16[256,16,896]{0,2,1:T(8,128)(2,1)}), bf16[256,16,896]{0,2,1:T(8,128)(2,1)}, u32[]{:S(2)}, u32[]{:S(2)}) async-start(bf16[256,16,896]{0,2,1:T(8,128)(2,1)} %bitcast.7), calls=%async_computation | async-start | bytes 14680064 | tf_op jit(solution)/shard_map/all_to_all | solution.py:137
  151.8 148.5 %all-gather.2.cloned.1.call-start = ((), (), s32[]{:S(2)}) async-start(), calls=%async_computation.2 | async-start | bytes 3342336 | tf_op jit(solution)/shard_map/all_gather | solution.py:128
  151.9 114.5 %collective-permute-start = (bf16[12,4096]{1,0:T(8,128)(2,1)S(1)}, bf16[12,4096]{1,0:T(8,128)(2,1)S(1)}, u32[]{:S(2)}, u32[]{:S(2)}) collective-permute-start(bf16[12,4096]{1,0:T(8,128)(2,1)S(1)} %constant_dynamic-slice_fusion.2), channel_id=1, source_target_pairs={{0,16},{1,17},{2,18},{3,19},{4,20},{5,21},{6,22},{7,23},{8,24},{9,... | collective-permute-start | bytes 294920 | tf_op jit(solution)/shard_map/ppermute | solution.py:125
  302.9 4.9 collective-permute-start.1
  319.4 6.2 %copy-start = (bf16[384,4096]{1,0:T(8,128)(2,1)S(1)}, bf16[384,4096]{1,0:T(8,128)(2,1)}, u32[]{:S(2)}) copy-start(bf16[384,4096]{1,0:T(8,128)(2,1)} %all-gather.2.cloned.1.call-done.a_ref) | copy-start | bytes 9437188
  403.9 120.8 %collective-permute-start.2 = (bf16[4,384,896]{2,1,0:T(8,128)(2,1)}, bf16[4,384,896]{2,1,0:T(8,128)(2,1)}, u32[]{:S(2)}, u32[]{:S(2)}) collective-permute-start(bf16[4,384,896]{2,1,0:T(8,128)(2,1)} %shard_map.50), channel_id=1, source_target_pairs={{0,16},{1,17},{2,18},{3,19},{4,20},{5,21},{6,22},{7,23},{8,24},{9,... | collective-permute-start | bytes 8257544 | tf_op jit(solution)/shard_map/ppermute | solution.py:152
Sparse Core Ops, SparseCore 0:
  267.3 32.9 all-gather.1
where the time goes:
time: 576 us; the launch traced here: 575 us
  waiting for transfers between devices  277 us (48%)
  Pallas kernels  157 us (27%)
  local copies, waits for them, and re-layouts  60.1 us (10%)
  blocking collectives  37.6 us (7%)
  starting transfers between devices  19.5 us (3%)
  between operations  14.1 us (2%)
  other arithmetic  9.37 us (2%)
    pallas_call x2, Pallas kernels, partial_residue(): pl.pallas_call(functools.partial(partial_kernel, steps), grid=(steps,), o...  157 us
    ppermute x1, waiting for transfers between devices, on_device(): other = lax.ppermute(away, 'dp', across)  112 us
    all_to_all x1, waiting for transfers between devices, on_device(): away_columns = exchange(away_weight)  102 us
    psum x1, blocking collectives, on_device(): totals = lax.psum(jnp.sum(column_sums, axis=1), ('dp', 'tensor'))  37.6 us
    all_gather x1, waiting for transfers between devices, on_device(): lax.all_gather(pair, 'dp', axis=0, tiled=True, axis_index_groups=groups)  33.1 us
    ppermute x1, waiting for transfers between devices, on_device(): arrived = lax.ppermute(away_part, 'dp', across)  27.6 us
    unnamed x6, local copies, waits for them, and re-layouts  20.2 us
  transfers between devices with their start and end apart: 6, of which 5 were waited for; matrix products, arithmetic and copies ran while one was open for 8% of the time, Pallas kernels for 27%

commit v1 on v0

--- a/solution.py
+++ b/solution.py
@@ -108,7 +108,7 @@
     )(tokens, columns, table)
 
 
-def on_device(activations, weight):
+def in_halves(activations, weight):
     n = lax.axis_size("dp")
     half = n // 2
     me = lax.axis_index("dp")
@@ -161,6 +161,386 @@
     return (own_mean, column_errors, errors)
 
 
+PLANES = 4
+CHUNK = 256
+BLOCK = 512
+AHEAD = 4
+BOW = (12.568868617017895, 50.02489230906822, 77.93933755195671)
+BOW_SHIFT = BOW[1] / (2.0 * BOW[2])
+BOW_FLOOR = BOW[0] / BOW[2] - BOW_SHIFT * BOW_SHIFT
+
+
+def change_of(w16, scale, unscale):
+    w = w16.astype(jnp.float32)
+    scaled = w if scale is None else w * scale
+    top = jnp.max(jnp.abs(scaled), axis=0, keepdims=True) + 1e-06
+    v = scaled * (7.0 / top)
+    r = v - jnp.round(v)
+    size = jnp.abs(r)
+    rest = 0.5 - size
+    m = size * rest + BOW_SHIFT
+    wave = (r * rest) * (m * m + BOW_FLOOR) * (top * (BOW[2] / (14.0 * math.pi)))
+    if unscale is not None:
+        wave = wave * unscale
+    return (w - wave).astype(jnp.bfloat16) - w16
+
+
+def fused_kernel(
+    n, a_ref, w_ref, mean_ref, col_ref, err_ref,
+    wbuf, abuf, astage, table, meanrow, change, acc, stage, recv, colsum, cbuf, mine, theirs, etile, etiles,
+    w_send, w_recv, az_send, az_recv, ab_send, ab_recv, mm_send, mm_recv, p_send, p_recv, c_send, c_recv, e_send, e_recv,
+):
+    depth = w_ref.shape[0]
+    plane = n // PLANES
+    channels = plane * depth
+    chunks = wbuf.shape[0]
+    half = chunks // 2
+    tokens = abuf.shape[0]
+    own = tokens // n
+    rows_each = own * PLANES
+    me = lax.axis_index("dp")
+    z, p = me // plane, me % plane
+    partner = p + 1 - 2 * (p % 2)
+
+    def copy_to(device, source, target, send, arrive):
+        return pltpu.make_async_remote_copy(
+            src_ref=source, dst_ref=target, send_sem=send, recv_sem=arrive,
+            device_id={"dp": device}, device_id_type=pl.DeviceIdType.MESH,
+        )
+
+    def settle(ref, sem):
+        pltpu.make_async_copy(ref, ref, sem).wait()
+
+    barrier = pltpu.get_barrier_semaphore()
+
+    @pl.loop(1, n)
+    def _(i):
+        pl.semaphore_signal(
+            barrier, inc=1, device_id={"dp": (me + i) % n}, device_id_type=pl.DeviceIdType.MESH
+        )
+
+    pl.semaphore_wait(barrier, n - 1)
+
+    def slab(at):
+        return a_ref.at[:, pl.ds(pl.multiple_of(at * channels, channels), channels)]
+
+    def z_copy(i):
+        to = (z + i) % PLANES
+        return copy_to(to * plane + p, slab(to), astage.at[z], az_send.at[i], az_recv.at[z])
+
+    for i in range(1, PLANES):
+        z_copy(i).start()
+    pltpu.make_async_copy(slab(z), astage.at[z], az_recv.at[z]).start()
+
+    def chunk_of(step):
+        return (step % 2) * half + step // 2
+
+    def send_weights(step):
+        c = chunk_of(step)
+        rows = pl.ds(pl.multiple_of(p * depth, depth), depth)
+
+        def piece(q):
+            at = pl.multiple_of((q * chunks + c) * CHUNK, CHUNK)
+            return w_ref.at[:, pl.ds(at, CHUNK)]
+
+        @pl.loop(1, plane)
+        def _(j):
+            q = (p + j) % plane
+            copy_to(z * plane + q, piece(q), wbuf.at[c, rows, :], w_send.at[c], w_recv.at[c]).start()
+
+        pltpu.make_async_copy(piece(p), wbuf.at[c, rows, :], w_recv.at[c]).start()
+
+    send_weights(0)
+
+    for i in range(PLANES):
+        settle(astage.at[i], az_recv.at[i])
+
+    def block(q):
+        return abuf.at[pl.ds(pl.multiple_of(q * rows_each, rows_each), rows_each), :]
+
+    @pl.loop(0, channels // LANES)
+    def _(i):
+        lanes = pl.ds(pl.multiple_of(i * LANES, LANES), LANES)
+        part = [astage[t, :, lanes].astype(jnp.float32)[:own] for t in range(PLANES)]
+        whole = jnp.concatenate(part, axis=0).astype(jnp.bfloat16)
+        abuf[pl.ds(pl.multiple_of(p * rows_each, rows_each), rows_each), lanes] = whole
+
+    for j in range(1, plane // 2):
+        to = (p + 2 * j) % plane
+        copy_to(z * plane + to, block(p), block(p), ab_send.at[j], ab_recv.at[p]).start()
+    copy_to(z * plane + partner, block(p), block(p), ab_send.at[0], ab_recv.at[p]).start()
+
+    for step in range(1, AHEAD):
+        send_weights(step)
+
+    for j in range(1, plane // 2):
+        q = (p + 2 * j) % plane
+        settle(block(q), ab_recv.at[q])
+        copy_to(z * plane + partner, block(q), block(q), ab_send.at[plane // 2 + j - 1], ab_recv.at[q]).start()
+    for j in range(plane // 2):
+        q = (partner + 2 * j) % plane
+        settle(block(q), ab_recv.at[q])
+
+    def means(i, carry):
+        most, least = carry
+        lanes = pl.ds(pl.multiple_of(i * LANES, LANES), LANES)
+        sums = jnp.sum(jnp.abs(abuf[:, lanes].astype(jnp.float32)), axis=0, keepdims=True)
+        mean = sums / tokens + 1e-06
+        meanrow[:, lanes] = mean
+        table[0, lanes, :] = jnp.transpose(jnp.broadcast_to(jnp.log(mean), (LANES, LANES)))
+        return jnp.maximum(most, mean), jnp.minimum(least, mean)
+
+    most, least = lax.fori_loop(
+        0, channels // LANES, means,
+        (jnp.zeros((1, LANES), jnp.float32), jnp.full((1, LANES), jnp.inf, jnp.float32)),
+    )
+    mean_ref[...] = meanrow[:, pl.ds(pl.multiple_of(p * depth, depth), depth)]
+    mine[0:1, :] = most
+    mine[1:2, :] = least
+
+    def mm_copy(i):
+        to = (z + i) % PLANES
+        return copy_to(to * plane + p, mine, theirs.at[i], mm_send.at[i], mm_recv.at[i])
+
+    for i in range(1, PLANES):
+        mm_copy(i).start()
+    for i in range(1, PLANES):
+        settle(theirs.at[i], mm_recv.at[i])
+        most = jnp.maximum(most, theirs[i, 0:1, :])
+        least = jnp.minimum(least, theirs[i, 1:2, :])
+    ends = jnp.log(jnp.max(most, axis=1, keepdims=True)) + jnp.log(jnp.min(least, axis=1, keepdims=True))
+    middle = 0.5 * ends
+
+    @pl.loop(0, channels // LANES)
+    def _(i):
+        rows = pl.ds(pl.multiple_of(i * LANES, LANES), LANES)
+        level = table[0, rows, :] - middle
+        for k in range(1, GRID):
+            table[2 * k - 2, rows, :] = jnp.exp((k / GRID) * level)
+            table[2 * k - 1, rows, :] = jnp.exp((-k / GRID) * level)
+
+    def partial_products(c):
+        acc[...] = jnp.zeros_like(acc)
+
+        @pl.loop(0, channels // BLOCK)
+        def _(b):
+            base = pl.multiple_of(b * BLOCK, BLOCK)
+            lhs = abuf[:, pl.ds(base, BLOCK)]
+            for k in range(GRID):
+                for g in range(BLOCK // GROUP):
+                    rows = pl.ds(base + g * GROUP, GROUP)
+                    for h in range(0, CHUNK, LANES):
+                        w16 = wbuf[c, rows, pl.ds(h, LANES)]
+                        scale = table[2 * k - 2, rows, :] if k else None
+                        unscale = table[2 * k - 1, rows, :] if k else None
+                        change[k, pl.ds(g * GROUP, GROUP), pl.ds(h, LANES)] = change_of(w16, scale, unscale)
+                acc[k] += jnp.dot(lhs, change[k], preferred_element_type=jnp.float32)
+
+    def hand_on(c, k, to):
+        return copy_to(to * plane + p, stage.at[c, k], recv.at[c, k], p_send.at[c, k], p_recv.at[c, k])
+
+    steps = chunks
+    for_side = ((PLANES - 1 - z, z - 1), (z, z + 1))
+
+    @pl.loop(0, steps + PLANES - 1)
+    def _(step):
+        @pl.when(step < steps)
+        def _():
+            c = chunk_of(step)
+
+            @pl.when(step + AHEAD < steps)
+            def _():
+                send_weights(step + AHEAD)
+
+            settle(wbuf.at[c], w_recv.at[c])
+            partial_products(c)
+            for k in range(GRID):
+                stage[c, k] = acc[k].astype(jnp.bfloat16)
+            for side in range(2):
+                gone, to = for_side[side]
+
+                @pl.when((step % 2 == side) & (gone == 0))
+                def _():
+                    for k in range(GRID):
+                        hand_on(c, k, to).start()
+
+        for side in range(2):
+            gone, to = for_side[side]
+            late = step - gone
+            c = side * half + (late + 2) // 2 - 1
+            ready = (gone > 0) & (late >= 0) & (late < steps) & ((late + 2) % 2 == side)
+
+            @pl.when(ready & (gone < PLANES - 1))
+            def _():
+                for k in range(GRID):
+                    settle(recv.at[c, k], p_recv.at[c, k])
+                    total = stage[c, k].astype(jnp.float32) + recv[c, k].astype(jnp.float32)
+                    stage[c, k] = total.astype(jnp.bfloat16)
+                    hand_on(c, k, to).start()
+
+            @pl.when(ready & (gone == PLANES - 1))
+            def _():
+                for k in range(GRID):
+                    settle(recv.at[c, k], p_recv.at[c, k])
+                    residue = stage[c, k].astype(jnp.float32) + recv[c, k].astype(jnp.float32)
+                    sums = jnp.sum(residue * residue, axis=0, keepdims=True)
+                    for h in range(0, CHUNK, LANES):
+                        at = c * CHUNK + h
+                        width = colsum.shape[2]
+                        lanes = pl.ds(pl.multiple_of(at % width, LANES), LANES)
+                        colsum[at // width, k : k + 1, lanes] = sums[:, h : h + LANES]
+
+    finishing = (z == 0) | (z == PLANES - 1)
+    first_block = jnp.where(z == 0, 0, PLANES // 2)
+    slot = jnp.where(z == 0, p, plane + p)
+
+    def column_copy(i):
+        j = first_block + i
+        return copy_to(p * PLANES + j, colsum.at[j], cbuf, c_send.at[i], c_recv)
+
+    def total_copy(i):
+        return copy_to((me + i) % n, etile, etiles.at[slot], e_send.at[i], e_recv.at[slot])
+
+    @pl.when(finishing)
+    def _():
+        for i in range(PLANES // 2):
+            to_self = p * PLANES + first_block + i == me
+
+            @pl.when(jnp.logical_not(to_self))
+            def _():
+                column_copy(i).start()
+
+            @pl.when(to_self)
+            def _():
+                cbuf[...] = colsum[first_block + i]
+
+        total = jnp.zeros((8, 1), jnp.float32)
+        for i in range(PLANES // 2):
+            total += jnp.sum(colsum[first_block + i], axis=1, keepdims=True)
+        etile[...] = jnp.broadcast_to(total, (8, LANES))
+        etiles[slot] = etile[...]
+
+        @pl.loop(1, n)
+        def _(i):
+            total_copy(i).start()
+
+    block_from, block_at = me // PLANES, me % PLANES
+    source = jnp.where(block_at < PLANES // 2, 0, PLANES - 1) * plane + block_from
+
+    @pl.when(source != me)
+    def _():
+        settle(cbuf, c_recv)
+
+    col_ref[...] = cbuf[...] * (1.0 / tokens)
+
+    @pl.loop(0, 2 * plane)
+    def _(i):
+        @pl.when(jnp.logical_not(finishing & (i == slot)))
+        def _():
+            settle(etiles.at[i], e_recv.at[i])
+
+    total = jnp.zeros((8, LANES), jnp.float32)
+    for i in range(2 * plane):
+        total += etiles[i]
+    err_ref[...] = total * (1.0 / (tokens * plane * chunks * CHUNK))
+
+    for i in range(1, PLANES):
+        z_copy(i).wait_send()
+        mm_copy(i).wait_send()
+    for i in range(plane - 1):
+        settle(block(0), ab_send.at[i])
+
+    @pl.loop(0, chunks)
+    def _(c):
+        settle(wbuf.at[0, pl.ds(0, channels - depth), :], w_send.at[c])
+
+        for side in range(2):
+            gone, to = for_side[side]
+
+            @pl.when((c // half == side) & (gone < PLANES - 1))
+            def _():
+                for k in range(GRID):
+                    settle(stage.at[c, k], p_send.at[c, k])
+
+    @pl.when(finishing)
+    def _():
+        for i in range(PLANES // 2):
+
+            @pl.when(p * PLANES + first_block + i != me)
+            def _():
+                settle(colsum.at[0], c_send.at[i])
+
+        @pl.loop(1, n)
+        def _(i):
+            settle(etile, e_send.at[i])
+
+
+def in_one_kernel(activations, weight):
+    n = lax.axis_size("dp")
+    own, depth = activations.shape[0], weight.shape[0]
+    plane = n // PLANES
+    channels, tokens = plane * depth, n * own
+    chunks = weight.shape[1] // (plane * CHUNK)
+    width = weight.shape[1] // n
+    padded = -(-own // 16) * 16
+    activations = jnp.pad(activations, ((0, padded - own), (0, 0)))
+    dma, f32, bf16 = pltpu.SemaphoreType.DMA, jnp.float32, jnp.bfloat16
+    mean, columns, errors = pl.pallas_call(
+        functools.partial(fused_kernel, n),
+        out_shape=(
+            jax.ShapeDtypeStruct((1, depth), f32),
+            jax.ShapeDtypeStruct((8, width), f32),
+            jax.ShapeDtypeStruct((8, LANES), f32),
+        ),
+        in_specs=[pl.BlockSpec(memory_space=pl.ANY)] * 2,
+        out_specs=[pl.BlockSpec(memory_space=pltpu.VMEM)] * 3,
+        scratch_shapes=[
+            pltpu.VMEM((chunks, channels, CHUNK), bf16),
+            pltpu.VMEM((tokens, channels), bf16),
+            pltpu.VMEM((PLANES, padded, channels), bf16),
+            pltpu.VMEM((2 * GRID - 2, channels, LANES), f32),
+            pltpu.VMEM((1, channels), f32),
+            pltpu.VMEM((GRID, BLOCK, CHUNK), bf16),
+            pltpu.VMEM((GRID, tokens, CHUNK), f32),
+            pltpu.VMEM((chunks, GRID, tokens, CHUNK), bf16),
+            pltpu.VMEM((chunks, GRID, tokens, CHUNK), bf16),
+            pltpu.VMEM((PLANES, 8, width), f32),
+            pltpu.VMEM((8, width), f32),
+            pltpu.VMEM((8, LANES), f32),
+            pltpu.VMEM((PLANES, 8, LANES), f32),
+            pltpu.VMEM((8, LANES), f32),
+            pltpu.VMEM((2 * plane, 8, LANES), f32),
+            dma((chunks,)), dma((chunks,)),
+            dma((PLANES,)), dma((PLANES,)),
+            dma((plane,)), dma((plane,)),
+            dma((PLANES,)), dma((PLANES,)),
+            dma((chunks, GRID)), dma((chunks, GRID)),
+            dma((PLANES // 2,)), dma,
+            dma((n,)), dma((2 * plane,)),
+        ],
+        compiler_params=pltpu.CompilerParams(
+            collective_id=0, has_side_effects=True, vmem_limit_bytes=62 << 20
+        ),
+    )(activations, weight)
+    return (mean.reshape(depth), columns[:GRID], errors[:GRID, 0])
+
+
+def one_kernel_fits(activations, weight):
+    n, tensor = lax.axis_size("dp"), lax.axis_size("tensor")
+    if tensor != 1 or n % (2 * PLANES) or n < 4 * PLANES:
+        return False
+    plane = n // PLANES
+    channels, width = plane * weight.shape[0], weight.shape[1]
+    aligned = (activations.shape[0] * PLANES) % 16 == 0 and weight.shape[0] % GROUP == 0
+    return aligned and channels % BLOCK == 0 and width % (2 * CHUNK * plane) == 0 and width % (LANES * n) == 0
+
+
+def on_device(activations, weight):
+    if one_kernel_fits(activations, weight):
+        return in_one_kernel(activations, weight)
+    return in_halves(activations, weight)
+
+
 def solution(mesh):
     placed = (P("dp", "tensor"), P("dp", "tensor"))
     return jax.shard_map(

time: 576 us -> 267 us (0.46)
  waiting for transfers between devices: 277 us -> 0 us
  Pallas kernels: 157 us -> 260 us
  local copies, waits for them, and re-layouts: 60.1 us -> 5.56 us
  blocking collectives: 37.6 us -> 0 us
  starting transfers between devices: 19.5 us -> 0 us
  between operations: 14.1 us -> 0.64 us
  other arithmetic: 9.37 us -> 0 us
    ppermute x3 -> x0, waiting for transfers between devices: 142 us -> none  [the longest x1 112 us: on_device(): other = lax.ppermute(away, 'dp', across)]
    pallas_call x2 -> x1, Pallas kernels: 157 us -> 260 us  [in_one_kernel(): pl.pallas_call(functools.partial(fused_kernel, n), out_shape=(jax.ShapeDt...]
    all_to_all x2 -> x0, waiting for transfers between devices: 102 us -> none  [the longest x1 102 us: on_device(): away_columns = exchange(away_weight)]
    psum x1 -> x0, blocking collectives: 37.6 us -> none  [on_device(): totals = lax.psum(jnp.sum(column_sums, axis=1), ('dp', 'tensor'))]
    all_gather x1 -> x0, waiting for transfers between devices: 33.1 us -> none  [on_device(): lax.all_gather(pair, 'dp', axis=0, tiled=True, axis_index_groups=groups)]
    all_to_all x2 -> x0, local copies, waits for them, and re-layouts: 22.4 us -> none  [the longest x1 11.2 us: on_device(): kept_columns = exchange(kept_weight)]
    unnamed x6 -> x1, local copies, waits for them, and re-layouts: 20.2 us -> 1.24 us
    all_to_all x2 -> x0, starting transfers between devices: 12.1 us -> none  [the longest x1 6.36 us: on_device(): away_columns = exchange(away_weight)]
  transfers between devices with their start and end apart: 6 -> 0, of which waited for: 5 -> 0; matrix products, arithmetic and copies ran while one was open for 8% -> 0% of each run, Pallas kernels for 27% -> 0%
where the time goes in v1:
time: 267 us; the launch traced here: 266 us
  Pallas kernels  260 us (97%)
  local copies, waits for them, and re-layouts  5.56 us (2%)
    pallas_call x1, Pallas kernels, in_one_kernel(): pl.pallas_call(functools.partial(fused_kernel, n), out_shape=(jax.ShapeDt...  260 us

profile of v1, /device:TPU:0, one launch (start us, length us, event | category | flops | bytes accessed | tf_op | source)
XLA Modules:
  0.0 266.3 jit_solution(4538494361044921130)
XLA Ops:
  0.6 1.7 pad.4.a_ref
  2.3 260.1 %shard_map.49 = (f32[1,256]{1,0:T(1,128)}, f32[8,896]{1,0:T(8,128)}, f32[8,128]{1,0:T(8,128)}) custom-call(bf16[16,8192]{1,0:T(8,128)(2,1)} %pad.4.a_ref, bf16[256,28672]{1,0:T(8,128)(2,1)} %w_ref.1), custom_call_target="tpu_custom_call" | custom-call | tf_op jit(solution)/shard_map/pallas_call | solution.py:488
  262.4 1.3 slice_reduce_fusion
  263.7 1.3 slice.6
  265.0 1.2 copy.6

commit v2 on v1

--- a/solution.py
+++ b/solution.py
@@ -162,9 +162,10 @@
 
 
 PLANES = 4
-CHUNK = 256
+CHUNK = 128
 BLOCK = 512
 AHEAD = 4
+LAG = 2
 BOW = (12.568868617017895, 50.02489230906822, 77.93933755195671)
 BOW_SHIFT = BOW[1] / (2.0 * BOW[2])
 BOW_FLOOR = BOW[0] / BOW[2] - BOW_SHIFT * BOW_SHIFT
@@ -261,7 +262,7 @@
     @pl.loop(0, channels // LANES)
     def _(i):
         lanes = pl.ds(pl.multiple_of(i * LANES, LANES), LANES)
-        part = [astage[t, :, lanes].astype(jnp.float32)[:own] for t in range(PLANES)]
+        part = [astage[t, :, lanes].astype(jnp.float32) for t in range(PLANES)]
         whole = jnp.concatenate(part, axis=0).astype(jnp.bfloat16)
         abuf[pl.ds(pl.multiple_of(p * rows_each, rows_each), rows_each), lanes] = whole
 
@@ -342,7 +343,7 @@
     steps = chunks
     for_side = ((PLANES - 1 - z, z - 1), (z, z + 1))
 
-    @pl.loop(0, steps + PLANES - 1)
+    @pl.loop(0, steps + LAG * (PLANES - 1))
     def _(step):
         @pl.when(step < steps)
         def _():
@@ -366,9 +367,9 @@
 
         for side in range(2):
             gone, to = for_side[side]
-            late = step - gone
-            c = side * half + (late + 2) // 2 - 1
-            ready = (gone > 0) & (late >= 0) & (late < steps) & ((late + 2) % 2 == side)
+            late = step - LAG * gone
+            c = side * half + late // 2
+            ready = (gone > 0) & (late >= 0) & (late < steps) & (step % 2 == side)
 
             @pl.when(ready & (gone < PLANES - 1))
             def _():
@@ -482,8 +483,6 @@
     channels, tokens = plane * depth, n * own
     chunks = weight.shape[1] // (plane * CHUNK)
     width = weight.shape[1] // n
-    padded = -(-own // 16) * 16
-    activations = jnp.pad(activations, ((0, padded - own), (0, 0)))
     dma, f32, bf16 = pltpu.SemaphoreType.DMA, jnp.float32, jnp.bfloat16
     mean, columns, errors = pl.pallas_call(
         functools.partial(fused_kernel, n),
@@ -497,7 +496,7 @@
         scratch_shapes=[
             pltpu.VMEM((chunks, channels, CHUNK), bf16),
             pltpu.VMEM((tokens, channels), bf16),
-            pltpu.VMEM((PLANES, padded, channels), bf16),
+            pltpu.VMEM((PLANES, own, channels), bf16),
             pltpu.VMEM((2 * GRID - 2, channels, LANES), f32),
             pltpu.VMEM((1, channels), f32),
             pltpu.VMEM((GRID, BLOCK, CHUNK), bf16),

time: 267 us -> 223 us (0.84)
  Pallas kernels: 260 us -> 218 us
    pallas_call x1, Pallas kernels: 260 us -> 218 us  [in_one_kernel(): pl.pallas_call(functools.partial(fused_kernel, n), out_shape=(jax.ShapeDt...]
where the time goes in v2:
time: 223 us
  Pallas kernels  218 us (98%)
  local copies, waits for them, and re-layouts  3.87 us (2%)
    pallas_call x1, Pallas kernels, in_one_kernel(): pl.pallas_call(functools.partial(fused_kernel, n), out_shape=(jax.ShapeDt...  218 us

profile of v2, /device:TPU:0, one launch (start us, length us, event | category | flops | bytes accessed | tf_op | source)
XLA Modules:
  0.0 222.5 jit_solution(1589473375290598289)
XLA Ops:
  0.6 218.0 %shard_map.49 = (f32[1,256]{1,0:T(1,128)}, f32[8,896]{1,0:T(8,128)}, f32[8,128]{1,0:T(8,128)}) custom-call(bf16[12,8192]{1,0:T(8,128)(2,1)} %a_ref.1, bf16[256,28672]{1,0:T(8,128)(2,1)} %w_ref.1), custom_call_target="tpu_custom_call" | custom-call | tf_op jit(solution)/shard_map/pallas_call | solution.py:487
  218.6 1.3 slice_reduce_fusion
  219.9 1.3 slice.6
  221.3 1.2 copy.6

commit v3 on v2

--- a/solution.py
+++ b/solution.py
@@ -162,10 +162,10 @@
 
 
 PLANES = 4
-CHUNK = 128
+CHUNK = LANES
 BLOCK = 512
 AHEAD = 4
-LAG = 2
+SKEW = 2
 BOW = (12.568868617017895, 50.02489230906822, 77.93933755195671)
 BOW_SHIFT = BOW[1] / (2.0 * BOW[2])
 BOW_FLOOR = BOW[0] / BOW[2] - BOW_SHIFT * BOW_SHIFT
@@ -188,14 +188,14 @@
 
 def fused_kernel(
     n, a_ref, w_ref, mean_ref, col_ref, err_ref,
-    wbuf, abuf, astage, table, meanrow, change, acc, stage, recv, colsum, cbuf, mine, theirs, etile, etiles,
-    w_send, w_recv, az_send, az_recv, ab_send, ab_recv, mm_send, mm_recv, p_send, p_recv, c_send, c_recv, e_send, e_recv,
+    wbuf, abuf, astage, table, meanrow, change, acc, stage, recv, colsum, cbuf, mine, theirs, etile, etiles, ztile, ztiles,
+    w_send, w_recv, az_send, az_recv, ab_send, ab_recv, mm_send, mm_recv, p_send, p_recv, c_send, c_recv, e_send, e_recv, t_send, t_recv,
 ):
     depth = w_ref.shape[0]
     plane = n // PLANES
     channels = plane * depth
     chunks = wbuf.shape[0]
-    half = chunks // 2
+    half, per = chunks // 2, chunks // PLANES
     tokens = abuf.shape[0]
     own = tokens // n
     rows_each = own * PLANES
@@ -214,13 +214,11 @@
 
     barrier = pltpu.get_barrier_semaphore()
 
-    @pl.loop(1, n)
-    def _(i):
-        pl.semaphore_signal(
-            barrier, inc=1, device_id={"dp": (me + i) % n}, device_id_type=pl.DeviceIdType.MESH
-        )
-
-    pl.semaphore_wait(barrier, n - 1)
+    near = [z * plane + (p + j) % plane for j in range(1, plane)]
+    near += [(z + i) % PLANES * plane + p for i in range(1, PLANES)]
+    for device in near:
+        pl.semaphore_signal(barrier, inc=1, device_id={"dp": device}, device_id_type=pl.DeviceIdType.MESH)
+    pl.semaphore_wait(barrier, len(near))
 
     def slab(at):
         return a_ref.at[:, pl.ds(pl.multiple_of(at * channels, channels), channels)]
@@ -233,15 +231,23 @@
         z_copy(i).start()
     pltpu.make_async_copy(slab(z), astage.at[z], az_recv.at[z]).start()
 
+    lead = jnp.where(z < PLANES // 2, 1, 0)
+    skew = jnp.where((z == 0) | (z == PLANES - 1), SKEW, 0)
+
     def chunk_of(step):
-        return (step % 2) * half + step // 2
+        early = step <= skew
+        late = step >= chunks - 1 - skew
+        even = (step + skew) % 2 == 0
+        side = jnp.where(early | (even & jnp.logical_not(late)), lead, 1 - lead)
+        middle = jnp.where(even, (step + skew) // 2, (step + chunks - skew - 1) // 2 - half)
+        return side * half + jnp.where(early, step, jnp.where(late, step - half, middle))
 
     def send_weights(step):
         c = chunk_of(step)
         rows = pl.ds(pl.multiple_of(p * depth, depth), depth)
 
         def piece(q):
-            at = pl.multiple_of((q * chunks + c) * CHUNK, CHUNK)
+            at = pl.multiple_of(((c // per) * plane * per + q * per + c % per) * CHUNK, CHUNK)
             return w_ref.at[:, pl.ds(at, CHUNK)]
 
         @pl.loop(1, plane)
@@ -320,22 +326,31 @@
             table[2 * k - 2, rows, :] = jnp.exp((k / GRID) * level)
             table[2 * k - 1, rows, :] = jnp.exp((-k / GRID) * level)
 
+    def add_product(pair, base):
+        lhs = abuf[:, pl.ds(base, BLOCK)]
+        acc[pair] += jnp.dot(lhs, change[pair], preferred_element_type=jnp.float32)
+
     def partial_products(c):
         acc[...] = jnp.zeros_like(acc)
+        change[1] = jnp.zeros_like(change[1])
 
         @pl.loop(0, channels // BLOCK)
         def _(b):
             base = pl.multiple_of(b * BLOCK, BLOCK)
-            lhs = abuf[:, pl.ds(base, BLOCK)]
-            for k in range(GRID):
-                for g in range(BLOCK // GROUP):
-                    rows = pl.ds(base + g * GROUP, GROUP)
-                    for h in range(0, CHUNK, LANES):
-                        w16 = wbuf[c, rows, pl.ds(h, LANES)]
+            add_product(1, pl.multiple_of(jnp.maximum(base - BLOCK, 0), BLOCK))
+            for pair in range(GRID // 2):
+                for k in (2 * pair, 2 * pair + 1):
+                    for g in range(BLOCK // GROUP):
+                        rows = pl.ds(base + g * GROUP, GROUP)
                         scale = table[2 * k - 2, rows, :] if k else None
                         unscale = table[2 * k - 1, rows, :] if k else None
-                        change[k, pl.ds(g * GROUP, GROUP), pl.ds(h, LANES)] = change_of(w16, scale, unscale)
-                acc[k] += jnp.dot(lhs, change[k], preferred_element_type=jnp.float32)
+                        change[pair, pl.ds(g * GROUP, GROUP), pl.ds(k % 2 * CHUNK, CHUNK)] = change_of(
+                            wbuf[c, rows, :], scale, unscale
+                        )
+                if pair == 0:
+                    add_product(0, base)
+
+        add_product(1, channels - BLOCK)
 
     def hand_on(c, k, to):
         return copy_to(to * plane + p, stage.at[c, k], recv.at[c, k], p_send.at[c, k], p_recv.at[c, k])
@@ -343,7 +358,7 @@
     steps = chunks
     for_side = ((PLANES - 1 - z, z - 1), (z, z + 1))
 
-    @pl.loop(0, steps + LAG * (PLANES - 1))
+    @pl.loop(0, steps - 1 + 2 * (PLANES - 2))
     def _(step):
         @pl.when(step < steps)
         def _():
@@ -356,20 +371,22 @@
             settle(wbuf.at[c], w_recv.at[c])
             partial_products(c)
             for k in range(GRID):
-                stage[c, k] = acc[k].astype(jnp.bfloat16)
+                stage[c, k] = acc[k // 2, :, k % 2 * CHUNK : (k % 2 + 1) * CHUNK].astype(jnp.bfloat16)
             for side in range(2):
                 gone, to = for_side[side]
 
-                @pl.when((step % 2 == side) & (gone == 0))
+                @pl.when((c // half == side) & (gone == 0))
                 def _():
                     for k in range(GRID):
                         hand_on(c, k, to).start()
 
         for side in range(2):
             gone, to = for_side[side]
-            late = step - LAG * gone
-            c = side * half + late // 2
-            ready = (gone > 0) & (late >= 0) & (late < steps) & (step % 2 == side)
+            turn = step - 2 * (gone - 1)
+            index = jnp.where(turn < 2 * SKEW, turn - SKEW, turn // 2)
+            c = side * half + index
+            due = (turn % 2 == 0) | (turn < 2 * SKEW)
+            ready = (gone > 0) & (turn >= SKEW) & due & (index < half)
 
             @pl.when(ready & (gone < PLANES - 1))
             def _():
@@ -393,19 +410,22 @@
 
     finishing = (z == 0) | (z == PLANES - 1)
     first_block = jnp.where(z == 0, 0, PLANES // 2)
-    slot = jnp.where(z == 0, p, plane + p)
+    end = jnp.where(z == 0, 0, 1)
 
     def column_copy(i):
         j = first_block + i
-        return copy_to(p * PLANES + j, colsum.at[j], cbuf, c_send.at[i], c_recv)
-
-    def total_copy(i):
-        return copy_to((me + i) % n, etile, etiles.at[slot], e_send.at[i], e_recv.at[slot])
+        return copy_to(j * plane + p, colsum.at[j], cbuf, c_send.at[i], c_recv)
+
+    def total_copy(j):
+        return copy_to(z * plane + (p + j) % plane, etile, etiles.at[p], e_send.at[j], e_recv.at[p])
+
+    def line_copy(i):
+        return copy_to((z + i) % PLANES * plane + p, ztile, ztiles.at[end], t_send.at[i], t_recv.at[end])
 
     @pl.when(finishing)
     def _():
         for i in range(PLANES // 2):
-            to_self = p * PLANES + first_block + i == me
+            to_self = first_block + i == z
 
             @pl.when(jnp.logical_not(to_self))
             def _():
@@ -419,31 +439,32 @@
         for i in range(PLANES // 2):
             total += jnp.sum(colsum[first_block + i], axis=1, keepdims=True)
         etile[...] = jnp.broadcast_to(total, (8, LANES))
-        etiles[slot] = etile[...]
-
-        @pl.loop(1, n)
-        def _(i):
-            total_copy(i).start()
-
-    block_from, block_at = me // PLANES, me % PLANES
-    source = jnp.where(block_at < PLANES // 2, 0, PLANES - 1) * plane + block_from
-
-    @pl.when(source != me)
+        for j in range(1, plane):
+            total_copy(j).start()
+        etiles[p] = etile[...]
+        for j in range(1, plane):
+            q = (p + j) % plane
+            settle(etiles.at[q], e_recv.at[q])
+        total = etiles[0]
+        for q in range(1, plane):
+            total += etiles[q]
+        ztile[...] = total
+        for i in range(1, PLANES):
+            line_copy(i).start()
+        ztiles[end] = total
+
+    @pl.when(jnp.logical_not(finishing))
     def _():
         settle(cbuf, c_recv)
 
     col_ref[...] = cbuf[...] * (1.0 / tokens)
-
-    @pl.loop(0, 2 * plane)
-    def _(i):
-        @pl.when(jnp.logical_not(finishing & (i == slot)))
+    for i in range(2):
+
+        @pl.when(z != i * (PLANES - 1))
         def _():
-            settle(etiles.at[i], e_recv.at[i])
-
-    total = jnp.zeros((8, LANES), jnp.float32)
-    for i in range(2 * plane):
-        total += etiles[i]
-    err_ref[...] = total * (1.0 / (tokens * plane * chunks * CHUNK))
+            settle(ztiles.at[i], t_recv.at[i])
+
+    err_ref[...] = (ztiles[0] + ztiles[1]) * (1.0 / (tokens * plane * chunks * CHUNK))
 
     for i in range(1, PLANES):
         z_copy(i).wait_send()
@@ -467,13 +488,14 @@
     def _():
         for i in range(PLANES // 2):
 
-            @pl.when(p * PLANES + first_block + i != me)
+            @pl.when(first_block + i != z)
             def _():
                 settle(colsum.at[0], c_send.at[i])
 
-        @pl.loop(1, n)
-        def _(i):
-            settle(etile, e_send.at[i])
+        for j in range(1, plane):
+            settle(etile, e_send.at[j])
+        for i in range(1, PLANES):
+            settle(ztile, t_send.at[i])
 
 
 def in_one_kernel(activations, weight):
@@ -499,8 +521,8 @@
             pltpu.VMEM((PLANES, own, channels), bf16),
             pltpu.VMEM((2 * GRID - 2, channels, LANES), f32),
             pltpu.VMEM((1, channels), f32),
-            pltpu.VMEM((GRID, BLOCK, CHUNK), bf16),
-            pltpu.VMEM((GRID, tokens, CHUNK), f32),
+            pltpu.VMEM((GRID // 2, BLOCK, 2 * CHUNK), bf16),
+            pltpu.VMEM((GRID // 2, tokens, 2 * CHUNK), f32),
             pltpu.VMEM((chunks, GRID, tokens, CHUNK), bf16),
             pltpu.VMEM((chunks, GRID, tokens, CHUNK), bf16),
             pltpu.VMEM((PLANES, 8, width), f32),
@@ -508,14 +530,17 @@
             pltpu.VMEM((8, LANES), f32),
             pltpu.VMEM((PLANES, 8, LANES), f32),
             pltpu.VMEM((8, LANES), f32),
-            pltpu.VMEM((2 * plane, 8, LANES), f32),
+            pltpu.VMEM((plane, 8, LANES), f32),
+            pltpu.VMEM((8, LANES), f32),
+            pltpu.VMEM((2, 8, LANES), f32),
             dma((chunks,)), dma((chunks,)),
             dma((PLANES,)), dma((PLANES,)),
             dma((plane,)), dma((plane,)),
             dma((PLANES,)), dma((PLANES,)),
             dma((chunks, GRID)), dma((chunks, GRID)),
             dma((PLANES // 2,)), dma,
-            dma((n,)), dma((2 * plane,)),
+            dma((plane,)), dma((plane,)),
+            dma((PLANES,)), dma((2,)),
         ],
         compiler_params=pltpu.CompilerParams(
             collective_id=0, has_side_effects=True, vmem_limit_bytes=62 << 20
@@ -531,7 +556,7 @@
     plane = n // PLANES
     channels, width = plane * weight.shape[0], weight.shape[1]
     aligned = (activations.shape[0] * PLANES) % 16 == 0 and weight.shape[0] % GROUP == 0
-    return aligned and channels % BLOCK == 0 and width % (2 * CHUNK * plane) == 0 and width % (LANES * n) == 0
+    return aligned and channels % BLOCK == 0 and width % (CHUNK * n) == 0
 
 
 def on_device(activations, weight):

time: 223 us -> 211 us (0.946)
  Pallas kernels: 218 us -> 206 us
    pallas_call x1, Pallas kernels: 218 us -> 206 us  [in_one_kernel(): pl.pallas_call(functools.partial(fused_kernel, n), out_shape=(jax.ShapeDt...]
where the time goes in v3:
time: 211 us
  Pallas kernels  206 us (98%)
  local copies, waits for them, and re-layouts  3.87 us (2%)
    pallas_call x1, Pallas kernels, in_one_kernel(): pl.pallas_call(functools.partial(fused_kernel, n), out_shape=(jax.ShapeDt...  206 us

profile of v3, /device:TPU:0, one launch (start us, length us, event | category | flops | bytes accessed | tf_op | source)
XLA Modules:
  0.0 210.9 jit_solution(14071590224363897248)
XLA Ops:
  0.6 206.4 %shard_map.49 = (f32[1,256]{1,0:T(1,128)}, f32[8,896]{1,0:T(8,128)}, f32[8,128]{1,0:T(8,128)}) custom-call(bf16[12,8192]{1,0:T(8,128)(2,1)} %a_ref.1, bf16[256,28672]{1,0:T(8,128)(2,1)} %w_ref.1), custom_call_target="tpu_custom_call" | custom-call | tf_op jit(solution)/shard_map/pallas_call | solution.py:509
  207.1 1.3 slice_reduce_fusion
  208.4 1.3 slice.6
  209.7 1.2 copy.6

commit v4 on v3

--- a/solution.py
+++ b/solution.py
@@ -166,6 +166,7 @@
 BLOCK = 512
 AHEAD = 4
 SKEW = 2
+EARLY = 4
 BOW = (12.568868617017895, 50.02489230906822, 77.93933755195671)
 BOW_SHIFT = BOW[1] / (2.0 * BOW[2])
 BOW_FLOOR = BOW[0] / BOW[2] - BOW_SHIFT * BOW_SHIFT
@@ -188,8 +189,8 @@
 
 def fused_kernel(
     n, a_ref, w_ref, mean_ref, col_ref, err_ref,
-    wbuf, abuf, astage, table, meanrow, change, acc, stage, recv, colsum, cbuf, mine, theirs, etile, etiles, ztile, ztiles,
-    w_send, w_recv, az_send, az_recv, ab_send, ab_recv, mm_send, mm_recv, p_send, p_recv, c_send, c_recv, e_send, e_recv, t_send, t_recv,
+    wbuf, abuf, astage, table, meanrow, change, acc, stage, recv, colsum, cbuf, mine, theirs, etile, etiles, ztile, ztiles, inward,
+    w_send, w_recv, az_send, az_recv, ab_send, ab_recv, mm_send, mm_recv, p_send, p_recv, c_send, c_recv, e_send, e_recv, t_send, t_recv, i_send, i_recv,
 ):
     depth = w_ref.shape[0]
     plane = n // PLANES
@@ -234,13 +235,19 @@
     lead = jnp.where(z < PLANES // 2, 1, 0)
     skew = jnp.where((z == 0) | (z == PLANES - 1), SKEW, 0)
 
+    def place_of(side, index):
+        return jnp.where(side == 0, index, chunks - 1 - index)
+
     def chunk_of(step):
         early = step <= skew
         late = step >= chunks - 1 - skew
         even = (step + skew) % 2 == 0
         side = jnp.where(early | (even & jnp.logical_not(late)), lead, 1 - lead)
         middle = jnp.where(even, (step + skew) // 2, (step + chunks - skew - 1) // 2 - half)
-        return side * half + jnp.where(early, step, jnp.where(late, step - half, middle))
+        index = jnp.where(early, step, jnp.where(late, step - half, middle))
+        moved = (skew > 0) & (side != lead) & (index >= half - EARLY)
+        index = jnp.where(moved, jnp.where(index == half - EARLY, half - 1, index - 1), index)
+        return place_of(side, index)
 
     def send_weights(step):
         c = chunk_of(step)
@@ -352,11 +359,17 @@
 
         add_product(1, channels - BLOCK)
 
+    def hand_inward(c, k, to):
+        return copy_to(to * plane + p, stage.at[c, k], inward.at[k], i_send.at[k], i_recv.at[k])
+
     def hand_on(c, k, to):
         return copy_to(to * plane + p, stage.at[c, k], recv.at[c, k], p_send.at[c, k], p_recv.at[c, k])
 
     steps = chunks
     for_side = ((PLANES - 1 - z, z - 1), (z, z + 1))
+    last_of = (half - 1, half)
+
+    colsum[...] = jnp.zeros_like(colsum)
 
     @pl.loop(0, steps - 1 + 2 * (PLANES - 2))
     def _(step):
@@ -380,15 +393,21 @@
                     for k in range(GRID):
                         hand_on(c, k, to).start()
 
+                @pl.when((c == last_of[side]) & (gone == PLANES - 1))
+                def _():
+                    for k in range(GRID):
+                        hand_inward(c, k, z + (1 - 2 * side)).start()
+
         for side in range(2):
             gone, to = for_side[side]
-            turn = step - 2 * (gone - 1)
+            turn = step - 2 * (gone - 1) - jnp.where(gone == PLANES - 1, 2, 0)
             index = jnp.where(turn < 2 * SKEW, turn - SKEW, turn // 2)
-            c = side * half + index
+            c = place_of(side, index)
+            inner_end = (index == half - 1) & (gone == PLANES - 2)
             due = (turn % 2 == 0) | (turn < 2 * SKEW)
             ready = (gone > 0) & (turn >= SKEW) & due & (index < half)
 
-            @pl.when(ready & (gone < PLANES - 1))
+            @pl.when(ready & (gone < PLANES - 1) & jnp.logical_not(inner_end))
             def _():
                 for k in range(GRID):
                     settle(recv.at[c, k], p_recv.at[c, k])
@@ -396,75 +415,77 @@
                     stage[c, k] = total.astype(jnp.bfloat16)
                     hand_on(c, k, to).start()
 
-            @pl.when(ready & (gone == PLANES - 1))
-            def _():
+            def finish(extra):
                 for k in range(GRID):
                     settle(recv.at[c, k], p_recv.at[c, k])
                     residue = stage[c, k].astype(jnp.float32) + recv[c, k].astype(jnp.float32)
+                    if extra:
+                        settle(inward.at[k], i_recv.at[k])
+                        residue += inward[k].astype(jnp.float32)
                     sums = jnp.sum(residue * residue, axis=0, keepdims=True)
-                    for h in range(0, CHUNK, LANES):
-                        at = c * CHUNK + h
-                        width = colsum.shape[2]
-                        lanes = pl.ds(pl.multiple_of(at % width, LANES), LANES)
-                        colsum[at // width, k : k + 1, lanes] = sums[:, h : h + LANES]
-
-    finishing = (z == 0) | (z == PLANES - 1)
-    first_block = jnp.where(z == 0, 0, PLANES // 2)
-    end = jnp.where(z == 0, 0, 1)
-
-    def column_copy(i):
-        j = first_block + i
-        return copy_to(j * plane + p, colsum.at[j], cbuf, c_send.at[i], c_recv)
+                    lanes = pl.ds(pl.multiple_of(c % per * CHUNK, CHUNK), CHUNK)
+                    colsum[c // per, k : k + 1, lanes] = sums
+
+            @pl.when(ready & (gone == PLANES - 1) & (index < half - 1))
+            def _():
+                finish(False)
+
+            @pl.when(ready & inner_end)
+            def _():
+                finish(True)
+
+    outer = (z == 0) | (z == PLANES - 1)
+    inner = jnp.where(z == 0, 1, PLANES - 2)
+
+    def column_copy():
+        return copy_to(inner * plane + p, colsum.at[inner], cbuf, c_send, c_recv)
 
     def total_copy(j):
         return copy_to(z * plane + (p + j) % plane, etile, etiles.at[p], e_send.at[j], e_recv.at[p])
 
     def line_copy(i):
-        return copy_to((z + i) % PLANES * plane + p, ztile, ztiles.at[end], t_send.at[i], t_recv.at[end])
-
-    @pl.when(finishing)
+        return copy_to((z + i) % PLANES * plane + p, ztile, ztiles.at[z], t_send.at[i], t_recv.at[z])
+
+    @pl.when(outer)
     def _():
-        for i in range(PLANES // 2):
-            to_self = first_block + i == z
-
-            @pl.when(jnp.logical_not(to_self))
-            def _():
-                column_copy(i).start()
-
-            @pl.when(to_self)
-            def _():
-                cbuf[...] = colsum[first_block + i]
-
-        total = jnp.zeros((8, 1), jnp.float32)
-        for i in range(PLANES // 2):
-            total += jnp.sum(colsum[first_block + i], axis=1, keepdims=True)
-        etile[...] = jnp.broadcast_to(total, (8, LANES))
-        for j in range(1, plane):
-            total_copy(j).start()
-        etiles[p] = etile[...]
-        for j in range(1, plane):
-            q = (p + j) % plane
-            settle(etiles.at[q], e_recv.at[q])
-        total = etiles[0]
-        for q in range(1, plane):
-            total += etiles[q]
-        ztile[...] = total
-        for i in range(1, PLANES):
-            line_copy(i).start()
-        ztiles[end] = total
-
-    @pl.when(jnp.logical_not(finishing))
+        column_copy().start()
+
+    total = jnp.zeros((8, 1), jnp.float32)
+    for i in range(PLANES):
+        total += jnp.sum(colsum[i], axis=1, keepdims=True)
+    etile[...] = jnp.broadcast_to(total, (8, LANES))
+    for j in range(1, plane):
+        total_copy(j).start()
+    etiles[p] = etile[...]
+    for j in range(1, plane):
+        q = (p + j) % plane
+        settle(etiles.at[q], e_recv.at[q])
+    total = etiles[0]
+    for q in range(1, plane):
+        total += etiles[q]
+    ztile[...] = total
+    for i in range(1, PLANES):
+        line_copy(i).start()
+    ztiles[z] = total
+
+    @pl.when(outer)
+    def _():
+        col_ref[...] = colsum[z] * (1.0 / tokens)
+
+    @pl.when(jnp.logical_not(outer))
     def _():
         settle(cbuf, c_recv)
-
-    col_ref[...] = cbuf[...] * (1.0 / tokens)
-    for i in range(2):
-
-        @pl.when(z != i * (PLANES - 1))
-        def _():
-            settle(ztiles.at[i], t_recv.at[i])
-
-    err_ref[...] = (ztiles[0] + ztiles[1]) * (1.0 / (tokens * plane * chunks * CHUNK))
+        col_ref[...] = (colsum[z] + cbuf[...]) * (1.0 / tokens)
+
+    for i in range(1, PLANES):
+        settle(ztiles.at[(z + i) % PLANES], t_recv.at[(z + i) % PLANES])
+    total = ztiles[0]
+    for i in range(1, PLANES):
+        total += ztiles[i]
+    on_lane = lax.broadcasted_iota(jnp.int32, (8, LANES), 0) == lax.broadcasted_iota(jnp.int32, (8, LANES), 1)
+    err_ref[...] = jnp.sum(jnp.where(on_lane, total, 0.0), axis=0, keepdims=True) * (
+        1.0 / (tokens * plane * chunks * CHUNK)
+    )
 
     for i in range(1, PLANES):
         z_copy(i).wait_send()
@@ -479,23 +500,30 @@
         for side in range(2):
             gone, to = for_side[side]
 
-            @pl.when((c // half == side) & (gone < PLANES - 1))
+            passed_on = (c // half == side) & (gone < PLANES - 1)
+            inner_end = (c == last_of[side]) & (gone == PLANES - 2)
+
+            @pl.when(passed_on & jnp.logical_not(inner_end))
             def _():
                 for k in range(GRID):
                     settle(stage.at[c, k], p_send.at[c, k])
 
-    @pl.when(finishing)
+    @pl.when(outer)
     def _():
-        for i in range(PLANES // 2):
-
-            @pl.when(first_block + i != z)
-            def _():
-                settle(colsum.at[0], c_send.at[i])
-
-        for j in range(1, plane):
-            settle(etile, e_send.at[j])
-        for i in range(1, PLANES):
-            settle(ztile, t_send.at[i])
+        for k in range(GRID):
+            settle(stage.at[0, k], i_send.at[k])
+        settle(cbuf, c_send)
+
+    for j in range(1, plane):
+        settle(etile, e_send.at[j])
+    for i in range(1, PLANES):
+        settle(ztile, t_send.at[i])
+
+
+def shape_results(mean_in, col_in, err_in, mean_ref, col_ref, err_ref):
+    mean_ref[...] = mean_in[0, :]
+    col_ref[...] = col_in[:GRID, :]
+    err_ref[...] = err_in[0, :GRID]
 
 
 def in_one_kernel(activations, weight):
@@ -511,7 +539,7 @@
         out_shape=(
             jax.ShapeDtypeStruct((1, depth), f32),
             jax.ShapeDtypeStruct((8, width), f32),
-            jax.ShapeDtypeStruct((8, LANES), f32),
+            jax.ShapeDtypeStruct((1, LANES), f32),
         ),
         in_specs=[pl.BlockSpec(memory_space=pl.ANY)] * 2,
         out_specs=[pl.BlockSpec(memory_space=pltpu.VMEM)] * 3,
@@ -532,21 +560,32 @@
             pltpu.VMEM((8, LANES), f32),
             pltpu.VMEM((plane, 8, LANES), f32),
             pltpu.VMEM((8, LANES), f32),
-            pltpu.VMEM((2, 8, LANES), f32),
+            pltpu.VMEM((PLANES, 8, LANES), f32),
+            pltpu.VMEM((GRID, tokens, CHUNK), bf16),
             dma((chunks,)), dma((chunks,)),
             dma((PLANES,)), dma((PLANES,)),
             dma((plane,)), dma((plane,)),
             dma((PLANES,)), dma((PLANES,)),
             dma((chunks, GRID)), dma((chunks, GRID)),
-            dma((PLANES // 2,)), dma,
+            dma, dma,
             dma((plane,)), dma((plane,)),
-            dma((PLANES,)), dma((2,)),
+            dma((PLANES,)), dma((PLANES,)),
+            dma((GRID,)), dma((GRID,)),
         ],
         compiler_params=pltpu.CompilerParams(
             collective_id=0, has_side_effects=True, vmem_limit_bytes=62 << 20
         ),
     )(activations, weight)
-    return (mean.reshape(depth), columns[:GRID], errors[:GRID, 0])
+    return pl.pallas_call(
+        shape_results,
+        out_shape=(
+            jax.ShapeDtypeStruct((depth,), f32),
+            jax.ShapeDtypeStruct((GRID, width), f32),
+            jax.ShapeDtypeStruct((GRID,), f32),
+        ),
+        in_specs=[pl.BlockSpec(memory_space=pltpu.VMEM)] * 3,
+        out_specs=[pl.BlockSpec(memory_space=pltpu.VMEM)] * 3,
+    )(mean, columns, errors)
 
 
 def one_kernel_fits(activations, weight):

time: 211 us -> 204 us (0.967)
  local copies, waits for them, and re-layouts: 3.87 us -> 0 us
  Pallas kernels: 206 us -> 203 us
    pallas_call x1, Pallas kernels: 206 us -> 201 us  [in_one_kernel(): pl.pallas_call(functools.partial(fused_kernel, n), out_shape=(jax.ShapeDt...]
    slice x2 -> x0, local copies, waits for them, and re-layouts: 2.65 us -> none  [in_one_kernel(): return (mean.reshape(depth), columns[:GRID], errors[:GRID, 0])]
where the time goes in v4:
time: 204 us; the launch traced here: 203 us
  Pallas kernels  203 us (100%)
    pallas_call x1, Pallas kernels, in_one_kernel(): pl.pallas_call(functools.partial(fused_kernel, n), out_shape=(jax.ShapeDt...  201 us

profile of v4, /device:TPU:0, one launch (start us, length us, event | category | flops | bytes accessed | tf_op | source)
XLA Modules:
  0.0 203.3 jit_solution(8419522470587673683)
XLA Ops:
  0.6 201.4 %shard_map.49 = (f32[1,256]{1,0:T(1,128)}, f32[8,896]{1,0:T(8,128)}, f32[1,128]{1,0:T(1,128)}) custom-call(bf16[12,8192]{1,0:T(8,128)(2,1)} %a_ref.1, bf16[256,28672]{1,0:T(8,128)(2,1)} %w_ref.1), custom_call_target="tpu_custom_call" | custom-call | tf_op jit(solution)/shard_map/pallas_call | solution.py:537
  202.0 1.4 shard_map.50

commit v5 on v4

--- a/solution.py
+++ b/solution.py
@@ -165,7 +165,7 @@
 CHUNK = LANES
 BLOCK = 512
 AHEAD = 4
-SKEW = 2
+SKEW = 3
 EARLY = 4
 BOW = (12.568868617017895, 50.02489230906822, 77.93933755195671)
 BOW_SHIFT = BOW[1] / (2.0 * BOW[2])
@@ -238,7 +238,12 @@
     def place_of(side, index):
         return jnp.where(side == 0, index, chunks - 1 - index)
 
+    def swapped(step, when):
+        return jnp.where(when & (step == chunks - 3), chunks - 2,
+                         jnp.where(when & (step == chunks - 2), chunks - 3, step))
+
     def chunk_of(step):
+        step = swapped(step, skew == 0)
         early = step <= skew
         late = step >= chunks - 1 - skew
         even = (step + skew) % 2 == 0
@@ -401,11 +406,12 @@
         for side in range(2):
             gone, to = for_side[side]
             turn = step - 2 * (gone - 1) - jnp.where(gone == PLANES - 1, 2, 0)
-            index = jnp.where(turn < 2 * SKEW, turn - SKEW, turn // 2)
+            turn = swapped(turn, gone == 1)
+            index = jnp.where(turn < 4, turn - 2, turn // 2)
             c = place_of(side, index)
             inner_end = (index == half - 1) & (gone == PLANES - 2)
-            due = (turn % 2 == 0) | (turn < 2 * SKEW)
-            ready = (gone > 0) & (turn >= SKEW) & due & (index < half)
+            due = (turn % 2 == 0) | (turn < 4)
+            ready = (gone > 0) & (turn >= 2) & due & (index < half)
 
             @pl.when(ready & (gone < PLANES - 1) & jnp.logical_not(inner_end))
             def _():

time: 204 us -> 197 us (0.966)
  Pallas kernels: 203 us -> 196 us
    pallas_call x1, Pallas kernels: 201 us -> 194 us  [in_one_kernel(): pl.pallas_call(functools.partial(fused_kernel, n), out_shape=(jax.ShapeDt...]
where the time goes in v5:
time: 197 us; the launch traced here: 196 us
  Pallas kernels  196 us (99%)
    pallas_call x1, Pallas kernels, in_one_kernel(): pl.pallas_call(functools.partial(fused_kernel, n), out_shape=(jax.ShapeDt...  194 us

profile of v5, /device:TPU:0, one launch (start us, length us, event | category | flops | bytes accessed | tf_op | source)
XLA Modules:
  0.0 196.3 jit_solution(7185743649592446270)
XLA Ops:
  0.6 194.3 %shard_map.49 = (f32[1,256]{1,0:T(1,128)}, f32[8,896]{1,0:T(8,128)}, f32[1,128]{1,0:T(1,128)}) custom-call(bf16[12,8192]{1,0:T(8,128)(2,1)} %a_ref.1, bf16[256,28672]{1,0:T(8,128)(2,1)} %w_ref.1), custom_call_target="tpu_custom_call" | custom-call | tf_op jit(solution)/shard_map/pallas_call | solution.py:543
  194.9 1.4 shard_map.50

commit v6 on v5

--- a/solution.py
+++ b/solution.py
@@ -351,8 +351,8 @@
             base = pl.multiple_of(b * BLOCK, BLOCK)
             add_product(1, pl.multiple_of(jnp.maximum(base - BLOCK, 0), BLOCK))
             for pair in range(GRID // 2):
-                for k in (2 * pair, 2 * pair + 1):
-                    for g in range(BLOCK // GROUP):
+                for g in range(BLOCK // GROUP):
+                    for k in (2 * pair, 2 * pair + 1):
                         rows = pl.ds(base + g * GROUP, GROUP)
                         scale = table[2 * k - 2, rows, :] if k else None
                         unscale = table[2 * k - 1, rows, :] if k else None

time: 197 us -> 196 us (level)
  no operation moved by 1% of the time
where the time goes in v6:
time: 196 us
  Pallas kernels  196 us (100%)
    pallas_call x1, Pallas kernels, in_one_kernel(): pl.pallas_call(functools.partial(fused_kernel, n), out_shape=(jax.ShapeDt...  194 us

profile of v6, /device:TPU:0, one launch (start us, length us, event | category | flops | bytes accessed | tf_op | source)
XLA Modules:
  0.0 196.3 jit_solution(6790218162889555629)
XLA Ops:
  0.6 194.3 %shard_map.49 = (f32[1,256]{1,0:T(1,128)}, f32[8,896]{1,0:T(8,128)}, f32[1,128]{1,0:T(1,128)}) custom-call(bf16[12,8192]{1,0:T(8,128)(2,1)} %a_ref.1, bf16[256,28672]{1,0:T(8,128)(2,1)} %w_ref.1), custom_call_target="tpu_custom_call" | custom-call | tf_op jit(solution)/shard_map/pallas_call | solution.py:543
  194.9 1.4 shard_map.50
